TPU v7x, 128 devices: a whole 4x4x4 slice. The times are simulated.
128 devices in a mesh: row: 16 (over x, z), col: 8 (over y, core).
Axes of the slice: x: 4, y: 4, z: 4, core: 2. Of those that a mesh axis runs over, the one named last changes fastest.
Arguments:
- front: float32 [9216, 9216], P('row', 'col')
- child_tiles: float32 [16384, 4096], P(('row', 'col')), may hold values from -0.4375 to 0.4375
- tile_target: int32 [16384], P(('row', 'col')), may hold values from 0 to 20735, as said below
- tile_count: int32 [512], P(('row', 'col')), may hold values from 24 to 32
- probe: float32 [9216, 512], P('col'), may hold values from -1.75 to 1.75
Outputs:
- panel_factor: float32 [9216, 1024], P('row', 'col')
- sketch: float32 [9216, 512], P('row', 'col')
Inputs may be any that keep to these rules, and one draw needn't show every extreme that they name: `tile_target`: among the 128 slots of one device, live or not, each counted once at its target tile and once at the mirrored tile, at most 2 placements fall inside the block of the front held by any one device.
All inputs are finite; a program needn't handle non-finite values.
Results may differ from a plain program's by a relative error of at most 0.00015.
Values sent between devices are 32-bit elements; how exact they have to be, the bound alone decides.
A program may use at most 128 MiB of HBM per device.

v0:
```python
import jax
import jax.numpy as jnp
from jax import lax
from jax.sharding import PartitionSpec as P

NB = 512
PANELS = 2
TB = 64
SLOTS = 32
HIGH = lax.Precision.HIGHEST


def in_blocks(value, dim, size):
    before, after = (value.shape[:dim], value.shape[dim + 1 :])
    return jnp.moveaxis(value.reshape(*before, size, -1, *after), dim, 0)


def joined_along(tiles, dim):
    lengths = list(tiles.shape[1:])
    lengths[dim] *= tiles.shape[0]
    return jnp.moveaxis(tiles, 0, dim).reshape(lengths)


def one_exchange(value, axis, axes, splits, concats):
    sizes = [lax.axis_size(a) for a in axes]
    tiles = in_blocks(value, splits[0], sizes[0])
    tiles = jnp.moveaxis(in_blocks(tiles, splits[1] + 1, sizes[1]), 0, 1)
    inside = tiles.shape[2:]
    tiles = tiles.reshape(-1, *inside)
    tiles = lax.all_to_all(tiles, axis, split_axis=0, concat_axis=0, tiled=True)
    tiles = joined_along(tiles.reshape(*sizes, *inside), concats[0] + 1)
    return joined_along(tiles, concats[1])


def filled_up(lines, size):
    spare = -lines.shape[0] % size
    if not spare:
        return lines
    return jnp.concatenate([lines, jnp.zeros((spare, *lines.shape[1:]), lines.dtype)])


def from_root(value, axis, root):
    lines = jnp.where(lax.axis_index(axis) == root, value, jnp.zeros_like(value)).reshape(
        -1, *value.shape[1:][-1:]
    )
    padded = filled_up(lines, lax.axis_size(axis))
    own = lax.psum_scatter(padded, axis, scatter_dimension=0, tiled=True)
    return lax.all_gather(own, axis, axis=0, tiled=True)[: len(lines)].reshape(value.shape)


def broadcast(value, axis, root):
    mine = lax.axis_index(axis) == root
    return lax.psum(jnp.where(mine, value, jnp.zeros_like(value)), axis)


def sum_at_owner(value, axis, dim):
    tiles = in_blocks(value, dim, lax.axis_size(axis))
    arrived = lax.all_to_all(tiles, axis, split_axis=0, concat_axis=0, tiled=True)
    return arrived.sum(axis=0)


def per_device(front, child_tiles, tile_target, tile_count, probe):
    row_count = lax.axis_size("row")
    col_count = lax.axis_size("col")
    devices = row_count * col_count
    local_rows, local_cols = front.shape
    tile_rows = local_rows // TB
    tile_cols = local_cols // TB
    grid = tile_cols * col_count
    local_tiles = tile_rows * tile_cols
    held = child_tiles.shape[0]
    capacity = 2 * max(1, (held + devices - 1) // devices)
    slot_index = jnp.arange(held, dtype=jnp.int32)
    live_once = slot_index % SLOTS < tile_count[slot_index // SLOTS]
    live = jnp.concatenate([live_once, live_once])
    mirrored = child_tiles.reshape(held, TB, TB).transpose(0, 2, 1).reshape(held, TB * TB)
    placements = jnp.concatenate([child_tiles, mirrored], axis=0)
    first_row = tile_target // grid
    first_col = tile_target % grid
    target_row = jnp.concatenate([first_row, first_col])
    target_col = jnp.concatenate([first_col, first_row])
    owner = target_row // tile_rows * col_count + target_col // tile_cols
    place = target_row % tile_rows * tile_cols + target_col % tile_cols
    onehot = (
        (owner[:, None] == jnp.arange(devices, dtype=jnp.int32)[None, :]) & live[:, None]
    ).astype(jnp.int32)
    earlier = jnp.cumsum(onehot, axis=0) - onehot
    rank = jnp.sum(earlier * onehot, axis=1)
    slot = jnp.where(live, owner * capacity + rank, devices * capacity)
    outgoing = (
        jnp.zeros((devices * capacity + 1, TB * TB), jnp.float32).at[slot].set(placements)[:-1]
    )
    where_to = jnp.full((devices * capacity + 1,), local_tiles, jnp.int32).at[slot].set(place)[:-1]
    shaped = (
        outgoing.reshape(row_count, col_count * capacity, TB * TB),
        where_to.reshape(row_count, col_count * capacity),
    )
    incoming, landing = (
        one_exchange(shaped[0], ("row", "col"), ("row", "col"), (0, 1), (0, 1)),
        one_exchange(shaped[1], ("row", "col"), ("row", "col"), (0, 1), (0, 1)),
    )
    incoming = incoming.reshape(-1, TB * TB)
    landing = landing.reshape(-1)
    extend = (
        jnp.zeros((local_tiles + 1, TB * TB), jnp.float32).at[landing].add(incoming)[:local_tiles]
    )
    extend = (
        extend.reshape(tile_rows, tile_cols, TB, TB)
        .transpose(0, 2, 1, 3)
        .reshape(local_rows, local_cols)
    )
    matrix = front + extend
    row_start = lax.axis_index("row") * local_rows
    col_start = lax.axis_index("col") * local_cols
    global_rows = row_start + jnp.arange(local_rows, dtype=jnp.int32)
    group = row_count // col_count
    margin = jnp.zeros((NB, NB), jnp.float32)
    factor_parts = []
    for k in range(PANELS):
        low = k * NB
        high = low + NB
        owner_col = low // local_cols
        offset = low % local_cols
        panel = from_root(matrix[:, offset : offset + NB], "col", owner_col)
        padded = jnp.concatenate([margin, panel, margin], axis=0)
        begin = jnp.clip(low - row_start + NB, 0, local_rows + NB)
        piece = lax.dynamic_slice_in_dim(padded, begin, NB, 0)
        diag_block = lax.psum(piece, "row")
        chol = jnp.linalg.cholesky(0.5 * (diag_block + diag_block.T))
        solved = jax.scipy.linalg.solve_triangular(chol, panel.T, lower=True).T
        factor_parts.append(jnp.where((global_rows >= low)[:, None], solved, 0.0))
        trail = jnp.where((global_rows >= high)[:, None], solved, 0.0)
        column_owner = lax.axis_index("col") * group
        pieces = [broadcast(trail, "row", column_owner + member) for member in range(group)]
        across = jnp.concatenate(pieces, axis=0)
        matrix = matrix - jnp.dot(trail, across.T, precision=HIGH)
    start = PANELS * NB
    global_cols = col_start + jnp.arange(local_cols, dtype=jnp.int32)
    weighted = jnp.where((global_cols >= start)[:, None], probe, 0.0)
    shares = sum_at_owner(
        lax.dot_general(weighted, matrix, (((0,), (1,)), ((), ())), precision=HIGH), "col", 0
    )
    sketch = jnp.where((global_rows >= start)[:, None], shares.T, 0.0)
    all_panels = jnp.concatenate(factor_parts, axis=1)
    width = all_panels.shape[1] // col_count
    panel_factor = lax.dynamic_slice_in_dim(all_panels, lax.axis_index("col") * width, width, 1)
    return (panel_factor, sketch)


def solution(mesh):
    return jax.shard_map(
        per_device,
        mesh=mesh,
        in_specs=(
            P("row", "col"),
            P(("row", "col"), None),
            P(("row", "col")),
            P(("row", "col")),
            P("col", None),
        ),
        out_specs=(P("row", "col"), P("row", "col")),
        check_vma=False,
    )
```

profile of v0, /device:TPU:1, one launch (start us, length us, event | category | flops | bytes accessed | tf_op | source)
XLA Modules:
  0.0 1003.4 jit_solution(17757820655012956910)
XLA Ops:
  17.6 11.5 %all-to-all-start = ((s32[128,1,2]{2,1,0:T(1,128)}), s32[128,1,2]{2,1,0:T(1,128)S(1)}, u32[]{:S(2)}, u32[]{:S(2)}) async-start(s32[128,1,2]{2,1,0:T(1,128)} %bitcast.16), calls=%async_computation | async-start | bytes 131072 | tf_op jit(solution)/shard_map/all_to_all | solution.py:30
  57.4 10.2 %all-to-all-start.1 = ((f32[128,1,2,4096]{3,2,1,0:T(2,128)}), f32[128,1,2,4096]{3,2,1,0:T(2,128)}, u32[]{:S(2)}, u32[]{:S(2)}) async-start(f32[128,1,2,4096]{3,2,1,0:T(2,128)} %bitcast.188), calls=%async_computation.1 | async-start | bytes 8388608 | tf_op jit(solution)/shard_map/all_to_all | solution.py:30
  68.0 52.1 %all-to-all-done.1 = f32[128,1,2,4096]{3,2,1,0:T(2,128)} async-done(((f32[128,1,2,4096]{3,2,1,0:T(2,128)}), f32[128,1,2,4096]{3,2,1,0:T(2,128)}, u32[]{:S(2)}, u32[]{:S(2)}) %all-to-all-start.1) | async-done | bytes 4194336 | tf_op jit(solution)/shard_map/all_to_all | solution.py:30
  157.8 27.1 %reduce-scatter.3.cloned.1.call-done = f32[72,512]{1,0:T(8,128)} async-done(((f32[576,512]{1,0:T(8,128)}), f32[72,512]{1,0:T(8,128)}) %reduce-scatter.3.cloned.1.call-update) | async-done | bytes 147472 | tf_op jit(solution)/shard_map/reduce_scatter | solution.py:47
  184.9 27.1 %all-gather.3.cloned.1.call-done = f32[576,512]{1,0:T(8,128)} async-done(((f32[72,512]{1,0:T(8,128)}), f32[576,512]{1,0:T(8,128)}) %all-gather.3.cloned.1.call-update) | async-done | bytes 1179664 | tf_op jit(solution)/shard_map/all_gather | solution.py:48
  216.5 84.9 %all-reduce.8.cloned.1.call-done = f32[512,512]{1,0:T(8,128)} async-done(((f32[512,512]{1,0:T(8,128)}), f32[512,512]{1,0:T(8,128)}) %all-reduce.8.cloned.1.call-update) | async-done | bytes 1048592 | tf_op jit(solution)/shard_map/psum | solution.py:128
  312.1 11.7 %cholesky.286 = f32[128,128]{1,0:T(8,128)S(1)} custom-call(f32[128,128]{1,0:T(8,128)S(1)} %cholesky.426), custom_call_target="Cholesky" | custom-call | tf_op jit(solution)/shard_map/jit(cholesky)/cholesky | solution.py:129
  338.0 11.7 %cholesky.305 = f32[128,128]{1,0:T(8,128)S(1)} custom-call(f32[128,128]{1,0:T(8,128)S(1)} %cholesky.430), custom_call_target="Cholesky" | custom-call | tf_op jit(solution)/shard_map/jit(cholesky)/cholesky | solution.py:129
  362.7 11.7 %cholesky.326 = f32[128,128]{1,0:T(8,128)S(1)} custom-call(f32[128,128]{1,0:T(8,128)S(1)} %cholesky.435), custom_call_target="Cholesky" | custom-call | tf_op jit(solution)/shard_map/jit(cholesky)/cholesky | solution.py:129
  387.8 12.1 %cholesky.343 = f32[128,128]{1,0:T(8,128)S(1)} custom-call(f32[128,128]{1,0:T(8,128)S(1)} %convolution_subtract_fusion.13), custom_call_target="Cholesky" | custom-call | tf_op jit(solution)/shard_map/jit(cholesky)/cholesky | solution.py:129
  406.8 11.9 %while.4 = (s32[]{:T(128)}, f32[512,512]{1,0:T(8,128)}, s32[4,2]{0,1:T(2,128)S(1)}, f32[4,128,128]{2,1,0:T(8,128)S(1)}, s32[]{:T(128)}) while((s32[]{:T(128)}, f32[512,512]{1,0:T(8,128)}, s32[4,2]{0,1:T(2,128)S(1)}, f32[4,128,128]{2,1,0:T(8,128)S(1)}, s32[]{:T(128)}) %tuple.68), condition=%wide.while_cond, body=%wide.while_body.sunk | while | flops 2 | bytes 131181 | solution.py:130
  418.8 39.3 %custom-call.30 = f32[4,128,128]{1,2,0:T(8,128)S(1)} custom-call(f32[4,128,128]{2,1,0:T(8,128)S(1)} %get-tuple-element.18), custom_call_target="InvertDiagBlocksLowerTriangular" | custom-call | tf_op jit(solution)/shard_map/jit(_solve_triangular)/triangular_solve | solution.py:130
  469.5 91.7 %all-reduce.14.cloned.1.call-done = (f32[576,512]{1,0:T(8,128)}, f32[576,512]{1,0:T(8,128)}) async-done(((f32[576,512]{1,0:T(8,128)}, f32[576,512]{1,0:T(8,128)}), (f32[576,512]{1,0:T(8,128)}, f32[576,512]{1,0:T(8,128)})) %all-reduce.14.cloned.1.call-update) | async-done | bytes 2359312 | tf_op jit(solution)/shard_map/psum | solution.py:53
  570.8 30.4 %reduce-scatter.5.cloned.1.call-done = f32[72,512]{1,0:T(8,128)} async-done(((f32[576,512]{1,0:T(8,128)}), f32[72,512]{1,0:T(8,128)}) %reduce-scatter.5.cloned.1.call-update) | async-done | bytes 147472 | tf_op jit(solution)/shard_map/reduce_scatter | solution.py:47
  601.3 26.9 %all-gather.5.cloned.1.call-done = f32[576,512]{1,0:T(8,128)} async-done(((f32[72,512]{1,0:T(8,128)}), f32[576,512]{1,0:T(8,128)}) %all-gather.5.cloned.1.call-update) | async-done | bytes 1179664 | tf_op jit(solution)/shard_map/all_gather | solution.py:48
  631.0 86.2 %all-reduce.10.cloned.1.call-done = f32[512,512]{1,0:T(8,128)} async-done(((f32[512,512]{1,0:T(8,128)}), f32[512,512]{1,0:T(8,128)}) %all-reduce.10.cloned.1.call-update) | async-done | bytes 1048592 | tf_op jit(solution)/shard_map/psum | solution.py:128
  720.1 11.7 %cholesky.358 = f32[128,128]{1,0:T(8,128)S(1)} custom-call(f32[128,128]{1,0:T(8,128)S(1)} %cholesky.439), custom_call_target="Cholesky" | custom-call | tf_op jit(solution)/shard_map/jit(cholesky)/cholesky | solution.py:129
  742.5 11.7 %cholesky.377 = f32[128,128]{1,0:T(8,128)S(1)} custom-call(f32[128,128]{1,0:T(8,128)S(1)} %cholesky.443), custom_call_target="Cholesky" | custom-call | tf_op jit(solution)/shard_map/jit(cholesky)/cholesky | solution.py:129
  766.4 11.7 %cholesky.398 = f32[128,128]{1,0:T(8,128)S(1)} custom-call(f32[128,128]{1,0:T(8,128)S(1)} %cholesky.448), custom_call_target="Cholesky" | custom-call | tf_op jit(solution)/shard_map/jit(cholesky)/cholesky | solution.py:129
  789.2 11.9 %cholesky.415 = f32[128,128]{1,0:T(8,128)S(1)} custom-call(f32[128,128]{1,0:T(8,128)S(1)} %convolution_subtract_fusion.12), custom_call_target="Cholesky" | custom-call | tf_op jit(solution)/shard_map/jit(cholesky)/cholesky | solution.py:129
  812.1 39.3 %custom-call.34 = f32[4,128,128]{1,2,0:T(8,128)S(1)} custom-call(f32[4,128,128]{2,1,0:T(8,128)S(1)} %get-tuple-element.19), custom_call_target="InvertDiagBlocksLowerTriangular" | custom-call | tf_op jit(solution)/shard_map/jit(_solve_triangular)/triangular_solve | solution.py:130
  859.8 91.7 %all-reduce.12.cloned.1.call-done = (f32[576,512]{1,0:T(8,128)}, f32[576,512]{1,0:T(8,128)}) async-done(((f32[576,512]{1,0:T(8,128)}, f32[576,512]{1,0:T(8,128)}), (f32[576,512]{1,0:T(8,128)}, f32[576,512]{1,0:T(8,128)})) %all-reduce.12.cloned.1.call-update) | async-done | bytes 2359312 | tf_op jit(solution)/shard_map/psum | solution.py:53
  958.6 12.7 %fusion.6 = f32[512,576]{1,0:T(8,128)} fusion(f32[576,1152]{1,0:T(8,128)S(1)} %convolution_subtract_fusion, f32[1152,512]{1,0:T(8,128)S(1)} %copy-done.12, pred[1152]{0:T(1024)(128)(4,1)S(1)} %add_compare_fusion), kind=kOutput, calls=%fused_computation.24 | convolution fusion | flops 4077453312 | bytes 6194304 | tf_op jit(solution)/shard_map/dot_general | solution.py:141
  978.6 17.0 %all-to-all-done.2 = f32[8,64,576]{2,1,0:T(8,128)S(1)} async-done(((f32[8,64,576]{2,1,0:T(8,128)}), f32[8,64,576]{2,1,0:T(8,128)S(1)}, u32[]{:S(2)}, u32[]{:S(2)}) %all-to-all-start.2) | async-done | bytes 1179680 | tf_op jit(solution)/shard_map/all_to_all | solution.py:58
  (195 shorter events, 248.6 us)
Async XLA Ops:
  17.6 39.7 %all-to-all-start = ((s32[128,1,2]{2,1,0:T(1,128)}), s32[128,1,2]{2,1,0:T(1,128)S(1)}, u32[]{:S(2)}, u32[]{:S(2)}) async-start(s32[128,1,2]{2,1,0:T(1,128)} %bitcast.16), calls=%async_computation | async-start | bytes 131072 | tf_op jit(solution)/shard_map/all_to_all | solution.py:30
  57.4 62.7 %all-to-all-start.1 = ((f32[128,1,2,4096]{3,2,1,0:T(2,128)}), f32[128,1,2,4096]{3,2,1,0:T(2,128)}, u32[]{:S(2)}, u32[]{:S(2)}) async-start(f32[128,1,2,4096]{3,2,1,0:T(2,128)} %bitcast.188), calls=%async_computation.1 | async-start | bytes 8388608 | tf_op jit(solution)/shard_map/all_to_all | solution.py:30
  67.6 117.3 %reduce-scatter.3.cloned.1.call-start = ((), (), s32[]{:S(2)}) async-start(), calls=%async_computation.5 | async-start | bytes 1327104 | tf_op jit(solution)/shard_map/reduce_scatter | solution.py:47
  157.7 54.3 %all-gather.3.cloned.1.call-start = ((), (), s32[]{:S(2)}) async-start(), calls=%async_computation.6 | async-start | bytes 1327104 | tf_op jit(solution)/shard_map/all_gather | solution.py:48
  184.9 116.6 %all-reduce.8.cloned.1.call-start = ((), (), s32[]{:S(2)}) async-start(), calls=%async_computation.7 | async-start | bytes 2097152 | tf_op jit(solution)/shard_map/psum | solution.py:128
  216.0 345.1 %all-reduce.14.cloned.1.call-start = ((), (), s32[]{:S(2)}) async-start(), calls=%async_computation.12 | async-start | bytes 4718592 | tf_op jit(solution)/shard_map/psum | solution.py:53
  311.1 1.0 copy-start.9
  458.1 3.3 copy-start.13
  458.1 3.3 copy-start.4
  467.3 2.1 copy-start.11
  469.4 131.8 %reduce-scatter.5.cloned.1.call-start = ((), (), s32[]{:S(2)}) async-start(), calls=%async_computation.8 | async-start | bytes 1327104 | tf_op jit(solution)/shard_map/reduce_scatter | solution.py:47
  568.0 1.5 copy-start
  570.7 57.5 %copy-start.3 = (f32[512,512]{1,0:T(8,128)S(1)}, f32[512,512]{1,0:T(8,128)}, u32[]{:S(2)}) copy-start(f32[512,512]{1,0:T(8,128)} %copy-done.2) | copy-start | bytes 3145732
  570.8 57.4 %all-gather.5.cloned.1.call-start = ((), (), s32[]{:S(2)}) async-start(), calls=%async_computation.9 | async-start | bytes 1327104 | tf_op jit(solution)/shard_map/all_gather | solution.py:48
  601.3 116.0 %all-reduce.10.cloned.1.call-start = ((), (), s32[]{:S(2)}) async-start(), calls=%async_computation.10 | async-start | bytes 2097152 | tf_op jit(solution)/shard_map/psum | solution.py:128
  630.8 320.8 %all-reduce.12.cloned.1.call-start = ((), (), s32[]{:S(2)}) async-start(), calls=%async_computation.11 | async-start | bytes 4718592 | tf_op jit(solution)/shard_map/psum | solution.py:53
  717.2 1.7 copy-start.7
  804.3 47.2 %copy-start.5 = (f32[576,512]{1,0:T(8,128)S(1)}, f32[576,512]{1,0:T(8,128)}, u32[]{:S(2)}) copy-start(f32[576,512]{1,0:T(8,128)} %all-gather.5.cloned.1.call-done) | copy-start | bytes 3538948
  812.1 39.3 %copy-start.8 = (f32[512,512]{1,0:T(8,128)}, f32[512,512]{1,0:T(8,128)S(1)}, u32[]{:S(2)}) copy-start(f32[512,512]{1,0:T(8,128)S(1)} %get-tuple-element.216) | copy-start | bytes 3145732
  857.6 2.1 copy-start.10
  857.7 93.9 %copy-start.1 = (f32[576,1152]{1,0:T(8,128)S(1)}, f32[576,1152]{1,0:T(8,128)}, u32[]{:S(2)}) copy-start(f32[576,1152]{1,0:T(8,128)} %copy-done) | copy-start | bytes 7962628
  951.6 7.0 copy-start.12
  971.3 6.5 copy-start.6
  971.3 24.3 %all-to-all-start.2 = ((f32[8,64,576]{2,1,0:T(8,128)}), f32[8,64,576]{2,1,0:T(8,128)S(1)}, u32[]{:S(2)}, u32[]{:S(2)}) async-start(f32[8,64,576]{2,1,0:T(8,128)} %bitcast.63), calls=%async_computation.4 | async-start | bytes 2621440 | tf_op jit(solution)/shard_map/all_to_all | solution.py:58
  (1 other events, 1.0 us)
Sparse Core Ops, SparseCore 0:
  157.8 26.9 reduce-scatter.2
  186.5 25.4 all-gather.2
  216.2 85.2 all-reduce.7
  469.5 91.5 all-reduce.13
  570.9 30.2 reduce-scatter.4
  602.8 25.3 all-gather.4
  631.4 85.7 all-reduce.9
  859.9 91.6 all-reduce.11
where the time goes:
time: 1010 us; the launch traced here: 1000 us
  waiting for transfers between devices  535 us (53%)
  other arithmetic  280 us (28%)
  local copies, waits for them, and re-layouts  87.2 us (9%)
  matrix products  51.5 us (5%)
  starting transfers between devices  29.3 us (3%)
  between operations  20 us (2%)
    psum x2, waiting for transfers between devices, broadcast(): return lax.psum(jnp.where(mine, value, jnp.zeros_like(value)), axis)  183 us
    psum x2, waiting for transfers between devices, per_device(): diag_block = lax.psum(piece, 'row')  171 us
    another operation x29, other arithmetic, per_device(): chol = jnp.linalg.cholesky(0.5 * (diag_block + diag_block.T))  160 us
    another operation x5, other arithmetic, per_device(): solved = jax.scipy.linalg.solve_triangular(chol, panel.T, lower=True).T  81.2 us
    reduce_scatter x2, waiting for transfers between devices, from_root(): own = lax.psum_scatter(padded, axis, scatter_dimension=0, tiled=True)  57.5 us
    all_gather x2, waiting for transfers between devices, from_root(): lax.all_gather(own, axis, axis=0, tiled=True)[:len(lines)]  53.9 us
    all_to_all x2, waiting for transfers between devices, one_exchange(): tiles = lax.all_to_all(tiles, axis, split_axis=0, concat_axis=0, tiled=True)  52.1 us
    all_to_all x2, starting transfers between devices, one_exchange(): tiles = lax.all_to_all(tiles, axis, split_axis=0, concat_axis=0, tiled=True)  21.7 us
  transfers between devices with their start and end apart: 11, of which 10 were waited for; matrix products, arithmetic and copies ran while one was open for 3% of the time, Pallas kernels for 0%

commit v1 on v0

--- a/solution.py
+++ b/solution.py
@@ -1,3 +1,4 @@
+import functools
 import jax
 import jax.numpy as jnp
 from jax import lax
@@ -8,6 +9,14 @@
 TB = 64
 SLOTS = 32
 HIGH = lax.Precision.HIGHEST
+
+
+def enter_slot_by_axis(t0, peer_axis):
+    t1 = lax.all_gather(t0, peer_axis)
+    return jnp.sum(t1, axis=0)
+
+
+attach_cells = functools.partial(enter_slot_by_axis, peer_axis="row")
 
 
 def in_blocks(value, dim, size):
@@ -125,7 +134,7 @@
         padded = jnp.concatenate([margin, panel, margin], axis=0)
         begin = jnp.clip(low - row_start + NB, 0, local_rows + NB)
         piece = lax.dynamic_slice_in_dim(padded, begin, NB, 0)
-        diag_block = lax.psum(piece, "row")
+        diag_block = attach_cells(piece)
         chol = jnp.linalg.cholesky(0.5 * (diag_block + diag_block.T))
         solved = jax.scipy.linalg.solve_triangular(chol, panel.T, lower=True).T
         factor_parts.append(jnp.where((global_rows >= low)[:, None], solved, 0.0))

time: 1010 us -> 1080 us (1.069)
  waiting for transfers between devices: 535 us -> 583 us
  other arithmetic: 280 us -> 297 us
    all_gather x0 -> x2, waiting for transfers between devices: none -> 221 us  [enter_slot_by_axis(): t1 = lax.all_gather(t0, peer_axis)]
    psum x2 -> x0, waiting for transfers between devices: 171 us -> none  [per_device(): diag_block = lax.psum(piece, 'row')]
    reduce_sum x0 -> x2, other arithmetic: none -> 16.9 us  [enter_slot_by_axis(): return jnp.sum(t1, axis=0)]
where the time goes in v1:
time: 1080 us; the launch traced here: 1070 us
  waiting for transfers between devices  583 us (54%)
  other arithmetic  297 us (28%)
  local copies, waits for them, and re-layouts  86.3 us (8%)
  matrix products  51.5 us (5%)
  starting transfers between devices  29.3 us (3%)
  between operations  20.2 us (2%)
    all_gather x2, waiting for transfers between devices, enter_slot_by_axis(): t1 = lax.all_gather(t0, peer_axis)  221 us
    psum x2, waiting for transfers between devices, broadcast(): return lax.psum(jnp.where(mine, value, jnp.zeros_like(value)), axis)  182 us
    another operation x29, other arithmetic, per_device(): chol = jnp.linalg.cholesky(0.5 * (diag_block + diag_block.T))  160 us
    another operation x5, other arithmetic, per_device(): solved = jax.scipy.linalg.solve_triangular(chol, panel.T, lower=True).T  81.2 us
    reduce_scatter x2, waiting for transfers between devices, from_root(): own = lax.psum_scatter(padded, axis, scatter_dimension=0, tiled=True)  57.5 us
    all_gather x2, waiting for transfers between devices, from_root(): lax.all_gather(own, axis, axis=0, tiled=True)[:len(lines)]  53.9 us
    all_to_all x2, waiting for transfers between devices, one_exchange(): tiles = lax.all_to_all(tiles, axis, split_axis=0, concat_axis=0, tiled=True)  52.1 us
    all_to_all x2, starting transfers between devices, one_exchange(): tiles = lax.all_to_all(tiles, axis, split_axis=0, concat_axis=0, tiled=True)  21.7 us
  transfers between devices with their start and end apart: 11, of which 10 were waited for; matrix products, arithmetic and copies ran while one was open for 3% of the time, Pallas kernels for 0%

profile of v1, /device:TPU:1, one launch (start us, length us, event | category | flops | bytes accessed | tf_op | source)
XLA Modules:
  0.0 1067.3 jit_solution(4312861428371530392)
XLA Ops:
  17.6 11.5 %all-to-all-start = ((s32[128,1,2]{2,1,0:T(1,128)}), s32[128,1,2]{2,1,0:T(1,128)S(1)}, u32[]{:S(2)}, u32[]{:S(2)}) async-start(s32[128,1,2]{2,1,0:T(1,128)} %bitcast.16), calls=%async_computation | async-start | bytes 131072 | tf_op jit(solution)/shard_map/all_to_all | solution.py:39
  57.4 10.2 all-to-all-start.1
  68.0 52.1 %all-to-all-done.1 = f32[128,1,2,4096]{3,2,1,0:T(2,128)} async-done(((f32[128,1,2,4096]{3,2,1,0:T(2,128)}), f32[128,1,2,4096]{3,2,1,0:T(2,128)}, u32[]{:S(2)}, u32[]{:S(2)}) %all-to-all-start.1) | async-done | bytes 4194336 | tf_op jit(solution)/shard_map/all_to_all | solution.py:39
  157.8 27.1 %reduce-scatter.3.cloned.1.call-done = f32[72,512]{1,0:T(8,128)} async-done(((f32[576,512]{1,0:T(8,128)}), f32[72,512]{1,0:T(8,128)}) %reduce-scatter.3.cloned.1.call-update) | async-done | bytes 147472 | tf_op jit(solution)/shard_map/reduce_scatter | solution.py:56
  184.9 27.1 %all-gather.7.cloned.1.call-done = f32[576,512]{1,0:T(8,128)} async-done(((f32[72,512]{1,0:T(8,128)}), f32[576,512]{1,0:T(8,128)}) %all-gather.7.cloned.1.call-update) | async-done | bytes 1179664 | tf_op jit(solution)/shard_map/all_gather | solution.py:57
  216.6 110.0 %all-gather.11.cloned.1.call-done = f32[8192,512]{1,0:T(8,128)} async-done(((f32[512,512]{1,0:T(8,128)}), f32[8192,512]{1,0:T(8,128)}) %all-gather.11.cloned.1.call-update) | async-done | bytes 16777232 | tf_op jit(solution)/shard_map/all_gather | solution.py:15
  346.2 11.7 %cholesky.286 = f32[128,128]{1,0:T(8,128)S(1)} custom-call(f32[128,128]{1,0:T(8,128)S(1)} %cholesky.426), custom_call_target="Cholesky" | custom-call | tf_op jit(solution)/shard_map/jit(cholesky)/cholesky | solution.py:138
  372.2 11.9 %cholesky.305 = f32[128,128]{1,0:T(8,128)S(1)} custom-call(f32[128,128]{1,0:T(8,128)S(1)} %cholesky.430), custom_call_target="Cholesky" | custom-call | tf_op jit(solution)/shard_map/jit(cholesky)/cholesky | solution.py:138
  396.9 11.7 %cholesky.326 = f32[128,128]{1,0:T(8,128)S(1)} custom-call(f32[128,128]{1,0:T(8,128)S(1)} %cholesky.435), custom_call_target="Cholesky" | custom-call | tf_op jit(solution)/shard_map/jit(cholesky)/cholesky | solution.py:138
  422.0 12.1 %cholesky.343 = f32[128,128]{1,0:T(8,128)S(1)} custom-call(f32[128,128]{1,0:T(8,128)S(1)} %convolution_subtract_fusion.13), custom_call_target="Cholesky" | custom-call | tf_op jit(solution)/shard_map/jit(cholesky)/cholesky | solution.py:138
  441.0 11.9 %while.4 = (s32[]{:T(128)}, f32[512,512]{1,0:T(8,128)}, s32[4,2]{0,1:T(2,128)S(1)}, f32[4,128,128]{2,1,0:T(8,128)S(1)}, s32[]{:T(128)}) while((s32[]{:T(128)}, f32[512,512]{1,0:T(8,128)}, s32[4,2]{0,1:T(2,128)S(1)}, f32[4,128,128]{2,1,0:T(8,128)S(1)}, s32[]{:T(128)}) %tuple.68), condition=%wide.while_cond, body=%wide.while_body.sunk | while | flops 2 | bytes 131181 | solution.py:139
  452.9 39.3 %custom-call.30 = f32[4,128,128]{1,2,0:T(8,128)S(1)} custom-call(f32[4,128,128]{2,1,0:T(8,128)S(1)} %get-tuple-element.18), custom_call_target="InvertDiagBlocksLowerTriangular" | custom-call | tf_op jit(solution)/shard_map/jit(_solve_triangular)/triangular_solve | solution.py:139
  503.7 90.8 %all-reduce.8.cloned.1.call-done = (f32[576,512]{1,0:T(8,128)}, f32[576,512]{1,0:T(8,128)}) async-done(((f32[576,512]{1,0:T(8,128)}, f32[576,512]{1,0:T(8,128)}), (f32[576,512]{1,0:T(8,128)}, f32[576,512]{1,0:T(8,128)})) %all-reduce.8.cloned.1.call-update) | async-done | bytes 2359312 | tf_op jit(solution)/shard_map/psum | solution.py:62
  604.1 30.4 %reduce-scatter.5.cloned.1.call-done = f32[72,512]{1,0:T(8,128)} async-done(((f32[576,512]{1,0:T(8,128)}), f32[72,512]{1,0:T(8,128)}) %reduce-scatter.5.cloned.1.call-update) | async-done | bytes 147472 | tf_op jit(solution)/shard_map/reduce_scatter | solution.py:56
  634.6 26.9 %all-gather.9.cloned.1.call-done = f32[576,512]{1,0:T(8,128)} async-done(((f32[72,512]{1,0:T(8,128)}), f32[576,512]{1,0:T(8,128)}) %all-gather.9.cloned.1.call-update) | async-done | bytes 1179664 | tf_op jit(solution)/shard_map/all_gather | solution.py:57
  664.4 110.6 %all-gather.13.cloned.1.call-done = f32[8192,512]{1,0:T(8,128)} async-done(((f32[512,512]{1,0:T(8,128)}), f32[8192,512]{1,0:T(8,128)}) %all-gather.13.cloned.1.call-update) | async-done | bytes 16777232 | tf_op jit(solution)/shard_map/all_gather | solution.py:15
  784.0 11.7 %cholesky.358 = f32[128,128]{1,0:T(8,128)S(1)} custom-call(f32[128,128]{1,0:T(8,128)S(1)} %cholesky.439), custom_call_target="Cholesky" | custom-call | tf_op jit(solution)/shard_map/jit(cholesky)/cholesky | solution.py:138
  806.4 12.1 %cholesky.377 = f32[128,128]{1,0:T(8,128)S(1)} custom-call(f32[128,128]{1,0:T(8,128)S(1)} %cholesky.443), custom_call_target="Cholesky" | custom-call | tf_op jit(solution)/shard_map/jit(cholesky)/cholesky | solution.py:138
  830.3 11.7 %cholesky.398 = f32[128,128]{1,0:T(8,128)S(1)} custom-call(f32[128,128]{1,0:T(8,128)S(1)} %cholesky.448), custom_call_target="Cholesky" | custom-call | tf_op jit(solution)/shard_map/jit(cholesky)/cholesky | solution.py:138
  853.1 11.9 %cholesky.415 = f32[128,128]{1,0:T(8,128)S(1)} custom-call(f32[128,128]{1,0:T(8,128)S(1)} %convolution_subtract_fusion.12), custom_call_target="Cholesky" | custom-call | tf_op jit(solution)/shard_map/jit(cholesky)/cholesky | solution.py:138
  876.9 39.3 %custom-call.34 = f32[4,128,128]{1,2,0:T(8,128)S(1)} custom-call(f32[4,128,128]{2,1,0:T(8,128)S(1)} %get-tuple-element.19), custom_call_target="InvertDiagBlocksLowerTriangular" | custom-call | tf_op jit(solution)/shard_map/jit(_solve_triangular)/triangular_solve | solution.py:139
  924.6 90.8 %all-reduce.6.cloned.1.call-done = (f32[576,512]{1,0:T(8,128)}, f32[576,512]{1,0:T(8,128)}) async-done(((f32[576,512]{1,0:T(8,128)}, f32[576,512]{1,0:T(8,128)}), (f32[576,512]{1,0:T(8,128)}, f32[576,512]{1,0:T(8,128)})) %all-reduce.6.cloned.1.call-update) | async-done | bytes 2359312 | tf_op jit(solution)/shard_map/psum | solution.py:62
  1022.5 12.7 %fusion.6 = f32[512,576]{1,0:T(8,128)} fusion(f32[576,1152]{1,0:T(8,128)S(1)} %convolution_subtract_fusion, f32[1152,512]{1,0:T(8,128)S(1)} %copy-done.11, pred[1152]{0:T(1024)(128)(4,1)S(1)} %add_compare_fusion), kind=kOutput, calls=%fused_computation.24 | convolution fusion | flops 4077453312 | bytes 6194304 | tf_op jit(solution)/shard_map/dot_general | solution.py:150
  1042.4 17.0 %all-to-all-done.2 = f32[8,64,576]{2,1,0:T(8,128)S(1)} async-done(((f32[8,64,576]{2,1,0:T(8,128)}), f32[8,64,576]{2,1,0:T(8,128)S(1)}, u32[]{:S(2)}, u32[]{:S(2)}) %all-to-all-start.2) | async-done | bytes 1179680 | tf_op jit(solution)/shard_map/all_to_all | solution.py:67
  (193 shorter events, 264.9 us)
Async XLA Ops:
  17.6 39.7 %all-to-all-start = ((s32[128,1,2]{2,1,0:T(1,128)}), s32[128,1,2]{2,1,0:T(1,128)S(1)}, u32[]{:S(2)}, u32[]{:S(2)}) async-start(s32[128,1,2]{2,1,0:T(1,128)} %bitcast.16), calls=%async_computation | async-start | bytes 131072 | tf_op jit(solution)/shard_map/all_to_all | solution.py:39
  57.4 62.7 %all-to-all-start.1 = ((f32[128,1,2,4096]{3,2,1,0:T(2,128)}), f32[128,1,2,4096]{3,2,1,0:T(2,128)}, u32[]{:S(2)}, u32[]{:S(2)}) async-start(f32[128,1,2,4096]{3,2,1,0:T(2,128)} %bitcast.194), calls=%async_computation.1 | async-start | bytes 8388608 | tf_op jit(solution)/shard_map/all_to_all | solution.py:39
  67.6 117.3 %reduce-scatter.3.cloned.1.call-start = ((), (), s32[]{:S(2)}) async-start(), calls=%async_computation.5 | async-start | bytes 1327104 | tf_op jit(solution)/shard_map/reduce_scatter | solution.py:56
  157.7 54.3 %all-gather.7.cloned.1.call-start = ((), (), s32[]{:S(2)}) async-start(), calls=%async_computation.6 | async-start | bytes 1327104 | tf_op jit(solution)/shard_map/all_gather | solution.py:57
  184.9 141.7 %all-gather.11.cloned.1.call-start = ((), (), s32[]{:S(2)}) async-start(), calls=%async_computation.9 | async-start | bytes 17825792 | tf_op jit(solution)/shard_map/all_gather | solution.py:15
  212.1 1.0 copy-start.2
  216.1 378.4 %all-reduce.8.cloned.1.call-start = ((), (), s32[]{:S(2)}) async-start(), calls=%async_computation.12 | async-start | bytes 4718592 | tf_op jit(solution)/shard_map/psum | solution.py:62
  345.2 1.0 copy-start.8
  492.3 3.3 copy-start.12
  492.3 3.3 copy-start.4
  501.5 2.1 copy-start.10
  503.6 130.9 %reduce-scatter.5.cloned.1.call-start = ((), (), s32[]{:S(2)}) async-start(), calls=%async_computation.7 | async-start | bytes 1327104 | tf_op jit(solution)/shard_map/reduce_scatter | solution.py:56
  601.3 1.5 copy-start
  604.0 57.5 %copy-start.3 = (f32[512,512]{1,0:T(8,128)S(1)}, f32[512,512]{1,0:T(8,128)}, u32[]{:S(2)}) copy-start(f32[512,512]{1,0:T(8,128)} %copy-done.2) | copy-start | bytes 3145732
  604.1 57.4 %all-gather.9.cloned.1.call-start = ((), (), s32[]{:S(2)}) async-start(), calls=%async_computation.8 | async-start | bytes 1327104 | tf_op jit(solution)/shard_map/all_gather | solution.py:57
  634.5 140.4 %all-gather.13.cloned.1.call-start = ((), (), s32[]{:S(2)}) async-start(), calls=%async_computation.10 | async-start | bytes 17825792 | tf_op jit(solution)/shard_map/all_gather | solution.py:15
  664.1 351.3 %all-reduce.6.cloned.1.call-start = ((), (), s32[]{:S(2)}) async-start(), calls=%async_computation.11 | async-start | bytes 4718592 | tf_op jit(solution)/shard_map/psum | solution.py:62
  868.2 48.0 %copy-start.5 = (f32[576,512]{1,0:T(8,128)S(1)}, f32[576,512]{1,0:T(8,128)}, u32[]{:S(2)}) copy-start(f32[576,512]{1,0:T(8,128)} %all-gather.9.cloned.1.call-done) | copy-start | bytes 3538948
  876.9 39.3 %copy-start.7 = (f32[512,512]{1,0:T(8,128)}, f32[512,512]{1,0:T(8,128)S(1)}, u32[]{:S(2)}) copy-start(f32[512,512]{1,0:T(8,128)S(1)} %get-tuple-element.216) | copy-start | bytes 3145732
  922.4 2.1 copy-start.9
  922.5 93.0 %copy-start.1 = (f32[576,1152]{1,0:T(8,128)S(1)}, f32[576,1152]{1,0:T(8,128)}, u32[]{:S(2)}) copy-start(f32[576,1152]{1,0:T(8,128)} %copy-done) | copy-start | bytes 7962628
  1015.4 7.0 copy-start.11
  1035.1 6.5 copy-start.6
  1035.1 24.3 %all-to-all-start.2 = ((f32[8,64,576]{2,1,0:T(8,128)}), f32[8,64,576]{2,1,0:T(8,128)S(1)}, u32[]{:S(2)}, u32[]{:S(2)}) async-start(f32[8,64,576]{2,1,0:T(8,128)} %bitcast.65), calls=%async_computation.4 | async-start | bytes 2621440 | tf_op jit(solution)/shard_map/all_to_all | solution.py:67
Sparse Core Ops, SparseCore 0:
  157.8 26.9 reduce-scatter.2
  186.5 25.4 all-gather.6
  216.2 110.3 all-gather.10
  503.7 90.6 all-reduce.7
  604.2 30.2 reduce-scatter.4
  636.1 25.3 all-gather.8
  664.2 110.6 all-gather.12
  924.7 90.6 all-reduce.5
